TPU v7x, 512 devices: a whole 4x4x16 slice. The times are simulated.
512 devices in a mesh: ref: 16 (over x, y_lo, core), dom: 32 (over z, y_hi).
Axes of the slice: x: 4, y: 4 (y_hi: 2, y_lo: 2; y = y_hi * 2 + y_lo), z: 16, core: 2. Of those that a mesh axis runs over, the one named last changes fastest.
Arguments:
- particles: bfloat16 [8192, 7168], P(('ref', 'dom')), may hold values from -16 to 16
- offsets: int32 [8192], P(('ref', 'dom')), may hold values from 0 to 8, as said below
- references: bfloat16 [512, 7168], P('ref'), may hold values from -0.6 to 0.6
- noise_weight: float32 [3584], replicated, may hold values from 0.06 to 0.24
- ref_class: int32 [512], replicated, may hold values from 0 to 7
- ref_orient: int32 [512], replicated, may hold values from 0 to 63
- class_logprior: float32 [8], replicated, may hold values from -1 to 1
- orient_logprior: float32 [64], replicated, may hold values from -1 to 1
Outputs:
- log_post: float32 [8192, 9, 512], P(('ref', 'dom'))
- class_sums: float32 [8, 7168], P(None, ('ref', 'dom'))
Inputs may be any that keep to these rules, and one draw needn't show every extreme that they name: `offsets`: index of the prior's centre: horizontal step (o mod 3) - 1 pixels, vertical step floor(o / 3) - 1 pixels.
All inputs are finite; a program needn't handle non-finite values.
Results may differ from a plain program's by a relative error of at most 0.0042.
Values may be sent and summed in bfloat16 or wider, within the bound.
A program may use at most 64 MiB of HBM per device.

v0:
```python
import math
import jax
import jax.numpy as jnp
from jax import lax
from jax.sharding import PartitionSpec as P

SHIFTS = 9


def in_blocks(shard, dim, length):
    before, after = (shard.shape[:dim], shard.shape[dim + 1 :])
    return jnp.moveaxis(shard.reshape(*before, length, -1, *after), dim, 0)


def sum_at_owner(shard, axis, dim):
    length = lax.axis_size(axis)
    blocks = lax.all_to_all(in_blocks(shard, dim, length), axis, 0, 0, tiled=True)
    return jnp.sum(blocks, axis=0)


def shift_tables(count):
    coeffs = jnp.arange(count, dtype=jnp.int32)
    column_freq = (coeffs % 56).astype(jnp.float32)
    row_freq = (coeffs // 56 - 32).astype(jnp.float32)
    shift_ids = jnp.arange(SHIFTS, dtype=jnp.int32)
    step_right = (shift_ids % 3 - 1).astype(jnp.float32)
    step_down = (shift_ids // 3 - 1).astype(jnp.float32)
    turning = (
        2.0
        * math.pi
        / 96.0
        * (step_right[:, None] * column_freq[None, :] + step_down[:, None] * row_freq[None, :])
    )
    return (jnp.cos(turning), jnp.sin(turning))


def centre_prior(offsets):
    shift_ids = jnp.arange(SHIFTS, dtype=jnp.int32)
    step_right = (shift_ids % 3 - 1).astype(jnp.float32)
    step_down = (shift_ids // 3 - 1).astype(jnp.float32)
    centre_right = (offsets % 3 - 1).astype(jnp.float32)
    centre_down = (offsets // 3 - 1).astype(jnp.float32)
    apart_right = step_right[None, :] - centre_right[:, None]
    apart_down = step_down[None, :] - centre_down[:, None]
    return -0.5 * (apart_right * apart_right + apart_down * apart_down)


def aligned_stack(real_part, imag_part, cosine_table, sine_table, twice):
    turned_real = (
        real_part[:, None, :] * cosine_table[None] - imag_part[:, None, :] * sine_table[None]
    )
    turned_imag = (
        real_part[:, None, :] * sine_table[None] + imag_part[:, None, :] * cosine_table[None]
    )
    stacked_rows = real_part.shape[0] * cosine_table.shape[0]
    scaled_real = (
        (turned_real * twice[None, None, :])
        .astype(jnp.bfloat16)
        .reshape(stacked_rows, real_part.shape[1])
    )
    scaled_imag = (
        (turned_imag * twice[None, None, :])
        .astype(jnp.bfloat16)
        .reshape(stacked_rows, real_part.shape[1])
    )
    return (scaled_real, scaled_imag)


def contract(left, right):
    return lax.dot_general(
        left, right, (((1,), (1,)), ((), ())), preferred_element_type=jnp.float32
    )


def local(
    particles,
    offsets,
    references,
    noise_weight,
    ref_class,
    ref_orient,
    class_logprior,
    orient_logprior,
):
    local_rows = particles.shape[0]
    coef_total = particles.shape[1] // 2
    ref_total = ref_class.shape[0]
    class_count = class_logprior.shape[0]
    cosine_table, sine_table = shift_tables(coef_total)
    twice = 2.0 * noise_weight
    values = particles.astype(jnp.float32)
    real_part = values[:, :coef_total]
    imag_part = values[:, coef_total:]
    scaled_real, scaled_imag = aligned_stack(real_part, imag_part, cosine_table, sine_table, twice)
    class_table = (ref_class[:, None] == jnp.arange(class_count, dtype=jnp.int32)[None, :]).astype(
        jnp.float32
    )
    orient_table = (
        ref_orient[:, None] == jnp.arange(orient_logprior.shape[0], dtype=jnp.int32)[None, :]
    ).astype(jnp.float32)
    prior = jnp.dot(class_table, class_logprior, precision=lax.Precision.HIGHEST) + jnp.dot(
        orient_table, orient_logprior, precision=lax.Precision.HIGHEST
    )
    segment = lax.all_gather(references, "ref", axis=0, tiled=True)
    cross_piece = contract(scaled_real, segment[:, :coef_total]) + contract(
        scaled_imag, segment[:, coef_total:]
    )
    wide = segment.astype(jnp.float32)
    norm_piece = jnp.sum(
        noise_weight[None, :]
        * (
            wide[:, :coef_total] * wide[:, :coef_total]
            + wide[:, coef_total:] * wide[:, coef_total:]
        ),
        axis=1,
    )
    scores = (
        cross_piece.reshape(local_rows, SHIFTS, ref_total)
        - norm_piece[None, None, :]
        + prior[None, None, :]
        + centre_prior(offsets)[:, :, None]
    )
    row_peak = jnp.max(scores, axis=(1, 2), keepdims=True)
    log_total = row_peak + jnp.log(jnp.sum(jnp.exp(scores - row_peak), axis=(1, 2), keepdims=True))
    log_post = scores - log_total
    class_post = jnp.dot(
        jnp.exp(log_post).reshape(local_rows * SHIFTS, ref_total),
        class_table,
        precision=lax.Precision.HIGHEST,
    ).reshape(local_rows, SHIFTS, class_count)
    sums_real = jnp.einsum("ntc,nk->tck", class_post, real_part, precision=lax.Precision.HIGHEST)
    sums_imag = jnp.einsum("ntc,nk->tck", class_post, imag_part, precision=lax.Precision.HIGHEST)
    class_real = jnp.einsum(
        "tk,tck->ck", cosine_table, sums_real, precision=lax.Precision.HIGHEST
    ) - jnp.einsum("tk,tck->ck", sine_table, sums_imag, precision=lax.Precision.HIGHEST)
    class_imag = jnp.einsum(
        "tk,tck->ck", sine_table, sums_real, precision=lax.Precision.HIGHEST
    ) + jnp.einsum("tk,tck->ck", cosine_table, sums_imag, precision=lax.Precision.HIGHEST)
    devices = lax.axis_size(("ref", "dom"))
    partial_value = jnp.concatenate([class_real, class_imag], axis=1) * (
        1.0 / math.sqrt(local_rows * devices)
    )
    by_ref = sum_at_owner(partial_value, "ref", 1)
    class_sums = sum_at_owner(by_ref, "dom", 1)
    return (log_post, class_sums)


def solution(mesh):
    return jax.shard_map(
        local,
        mesh=mesh,
        in_specs=(
            P(("ref", "dom"), None),
            P(("ref", "dom")),
            P("ref", None),
            P(),
            P(),
            P(),
            P(),
            P(),
        ),
        out_specs=(P(("ref", "dom"), None, None), P(None, ("ref", "dom"))),
        check_vma=False,
    )
```

profile of v0, /device:TPU:32, one launch (start us, length us, event | category | flops | bytes accessed | tf_op | source)
XLA Modules:
  0.0 147.3 jit_solution(8516085216977881511)
XLA Ops:
  7.2 0.7 all-gather.2.cloned.1.call-update
  7.9 0.1 sub.250
  8.0 0.7 fusion.43
  8.7 0.1 sub.241
  8.8 0.1 sub.251
  8.9 0.1 sub.246
  9.0 0.1 sub.236
  9.0 0.1 sub.247
  9.2 1.0 fusion.46
  10.1 1.6 %fusion.23 = (f32[3584,9]{0,1:T(8,128)S(1)}, f32[3584,9]{0,1:T(8,128)}, f32[9,3584]{1,0:T(8,128)S(1)}, f32[9,3584]{1,0:T(8,128)S(1)}) fusion(f32[3584]{0:T(1024)S(1)} %get-tuple-element.26, f32[9]{0:T(128)S(1)} %get-tuple-element.29, f32[3584]{0:T(1024)S(1)} %get-tuple-element.27, f32[9]{0:T(128)S(1)} %get-tuple-element.28), kind=kLoop, calls=%fused_computation.43 | loop fusion | flops 129024 | bytes 544840
  11.7 4.0 %multiply_subtract_fusion = (f32[16,9,3584]{2,1,0:T(8,128)}, f32[16,9,3584]{2,1,0:T(8,128)}) fusion(f32[9,3584]{1,0:T(8,128)S(1)} %get-tuple-element.20, f32[16,3584]{1,0:T(8,128)S(1)} %get-tuple-element.17, f32[9,3584]{1,0:T(8,128)S(1)} %get-tuple-element.21, f32[16,3584]{1,0:T(8,128)S(1)} %get-tuple-element.16), kind=kLoop, calls=%fused_computation.12 | loop fusion | flops 3096576 | bytes 4845568 | tf_op jit(solution)/shard_map/sub | solution.py:50
  15.7 3.2 %add.202 = f32[144,3584]{1,0:T(8,128)} reshape(f32[16,9,3584]{2,1,0:T(8,128)} %get-tuple-element.15) | data formatting | bytes 4128768 | tf_op jit(solution)/shard_map/add | solution.py:53
  19.0 2.3 %sub.231 = f32[144,3584]{1,0:T(8,128)S(1)} reshape(f32[16,9,3584]{2,1,0:T(8,128)} %get-tuple-element.14) | data formatting | bytes 4128768 | tf_op jit(solution)/shard_map/sub | solution.py:50
  21.3 0.1 fusion.29
  21.4 0.3 fusion.13
  21.8 47.2 %all-gather.2.cloned.1.call-done = bf16[512,7168]{1,0:T(8,128)(2,1)} async-done(((bf16[32,7168]{1,0:T(8,128)(2,1)}), bf16[512,7168]{1,0:T(8,128)(2,1)}) %all-gather.2.cloned.1.call-update) | async-done | bytes 7340048 | tf_op jit(solution)/shard_map/all_gather | solution.py:104
  69.0 10.2 %convert_element_type.131 = f32[512,7168]{1,0:T(8,128)} convert(bf16[512,7168]{1,0:T(8,128)(2,1)} %all-gather.2.cloned.1.call-done) | non-fusion elementwise | flops 3670016 | bytes 22020096 | tf_op jit(solution)/shard_map/convert_element_type | solution.py:108
  79.3 6.1 %fusion.2 = f32[512]{0:T(512)S(1)} fusion(f32[512,7168]{1,0:T(8,128)} %convert_element_type.131, f32[3584]{0:T(1024)S(1)} %copy-done.5), kind=kLoop, calls=%fused_computation.3 | loop fusion | flops 9174528 | bytes 14696448 | tf_op jit(solution)/shard_map/reduce_sum | solution.py:109
  85.3 1.2 copy-done.1
  86.6 0.6 copy-done.3
  87.2 1.3 fusion.3
  88.5 1.5 %fusion.16 = (f32[144]{0:T(256)S(1)}, f32[144,512]{1,0:T(8,128)S(1)}) fusion(f32[144]{0:T(256)S(1)} %add_multiply_fusion.2, f32[512]{0:T(512)S(1)} %add.205, f32[512]{0:T(512)S(1)} %fusion.2, f32[144,512]{1,0:T(8,128)S(1)} %fusion.3, bf16[512,7168]{1,0:T(8,128)(2,1)S(1)} %copy-done.1, f32[144,3584]{1,0:T(8,128)S(1)} %sub.231, ...), kind=kOutput, calls=%fused_computation.34 | convolution fusion | flops 529883008 | bytes 6346304 | tf_op jit(solution)/shard_map/dot_general | solution.py:70
  90.0 0.1 reduce_max.14
  90.1 0.1 reduce_max.18
  90.2 0.1 sub.253
  90.3 0.1 sub.254
  90.4 0.2 exponential_reduce_fusion
  90.6 0.1 reduce_sum.45
  90.7 0.1 reduce_sum.46
  90.9 0.1 sub.260
  91.0 0.1 subtract_exponential_fusion
  91.2 1.0 fusion.34
  92.2 0.1 copy.19
  92.4 0.5 convolution_bitcast_fusion
  92.9 0.7 multiply_reduce_fusion.3
  93.7 0.1 concatenate.9
  93.8 0.1 concatenate.8
  94.0 0.9 fusion.12
  94.8 5.0 %all-to-all-start = ((f32[16,8,448]{2,1,0:T(8,128)}), f32[16,8,448]{2,1,0:T(8,128)S(1)}, u32[]{:S(2)}, u32[]{:S(2)}) async-start(f32[16,8,448]{2,1,0:T(8,128)} %fusion.12), calls=%async_computation | async-start | bytes 524288 | tf_op jit(solution)/shard_map/all_to_all | solution.py:17
  99.8 0.1 add_multiply_fusion.1
  99.9 7.5 %all-to-all-done = f32[16,8,448]{2,1,0:T(8,128)S(1)} async-done(((f32[16,8,448]{2,1,0:T(8,128)}), f32[16,8,448]{2,1,0:T(8,128)S(1)}, u32[]{:S(2)}, u32[]{:S(2)}) %all-to-all-start) | async-done | bytes 229408 | tf_op jit(solution)/shard_map/all_to_all | solution.py:17
  107.5 0.1 reshape.307
  107.7 0.7 copy.22
  108.4 15.0 %all-to-all-start.1 = ((f32[32,8,14]{2,1,0:T(8,128)}), f32[32,8,14]{2,1,0:T(8,128)S(1)}, u32[]{:S(2)}, u32[]{:S(2)}) async-start(f32[32,8,14]{2,1,0:T(8,128)} %copy.22), calls=%async_computation.1 | async-start | bytes 262144 | tf_op jit(solution)/shard_map/all_to_all | solution.py:17
  123.3 0.1 add_subtract_fusion
  123.5 0.9 copy.23
  124.4 15.4 %all-to-all-done.1 = f32[32,8,14]{2,1,0:T(8,128)S(1)} async-done(((f32[32,8,14]{2,1,0:T(8,128)}), f32[32,8,14]{2,1,0:T(8,128)S(1)}, u32[]{:S(2)}, u32[]{:S(2)}) %all-to-all-start.1) | async-done | bytes 14368 | tf_op jit(solution)/shard_map/all_to_all | solution.py:17
  139.8 0.6 reduce_sum.48
  (32 shorter events, 0.4 us)
Async XLA Ops:
  7.2 14.1 %copy-start = (f32[8]{0:T(128)S(1)}, f32[8]{0:T(128)}, u32[]{:S(2)}) copy-start(f32[8]{0:T(128)} %param.14) | copy-start | bytes 100
  7.2 61.9 %all-gather.2.cloned.1.call-start = ((), (), s32[]{:S(2)}) async-start(), calls=%async_computation.2 | async-start | bytes 7798784 | tf_op jit(solution)/shard_map/all_gather | solution.py:104
  19.0 2.3 %copy-start.6 = (s32[512]{0:T(512)S(1)}, s32[512]{0:T(512)}, u32[]{:S(2)}) copy-start(s32[512]{0:T(512)} %param.12) | copy-start | bytes 6148
  19.0 2.5 %copy-start.7 = (s32[512]{0:T(512)S(1)}, s32[512]{0:T(512)}, u32[]{:S(2)}) copy-start(s32[512]{0:T(512)} %param.13) | copy-start | bytes 6148
  19.0 2.5 %copy-start.8 = (f32[64]{0:T(128)S(1)}, f32[64]{0:T(128)}, u32[]{:S(2)}) copy-start(f32[64]{0:T(128)} %param.15) | copy-start | bytes 772
  19.0 2.8 %copy-start.5 = (f32[3584]{0:T(1024)S(1)}, f32[3584]{0:T(1024)}, u32[]{:S(2)}) copy-start(f32[3584]{0:T(1024)} %param.11) | copy-start | bytes 43012
  79.3 7.3 %copy-start.1 = (bf16[512,7168]{1,0:T(8,128)(2,1)S(1)}, bf16[512,7168]{1,0:T(8,128)(2,1)}, u32[]{:S(2)}) copy-start(bf16[512,7168]{1,0:T(8,128)(2,1)} %all-gather.2.cloned.1.call-done) | copy-start | bytes 22020100
  79.3 7.9 %copy-start.3 = (f32[144,3584]{1,0:T(8,128)S(1)}, f32[144,3584]{1,0:T(8,128)}, u32[]{:S(2)}) copy-start(f32[144,3584]{1,0:T(8,128)} %add.202) | copy-start | bytes 6193156
  88.5 3.9 %copy-start.2 = (bf16[16,7168]{1,0:T(8,128)(2,1)S(1)}, bf16[16,7168]{1,0:T(8,128)(2,1)}, u32[]{:S(2)}) copy-start(bf16[16,7168]{1,0:T(8,128)(2,1)} %param.8) | copy-start | bytes 688132
  90.0 2.9 %copy-start.4 = (f32[3584,9]{0,1:T(8,128)S(1)}, f32[3584,9]{0,1:T(8,128)}, u32[]{:S(2)}) copy-start(f32[3584,9]{0,1:T(8,128)} %get-tuple-element.19) | copy-start | bytes 387076
  94.8 12.6 %all-to-all-start = ((f32[16,8,448]{2,1,0:T(8,128)}), f32[16,8,448]{2,1,0:T(8,128)S(1)}, u32[]{:S(2)}, u32[]{:S(2)}) async-start(f32[16,8,448]{2,1,0:T(8,128)} %fusion.12), calls=%async_computation | async-start | bytes 524288 | tf_op jit(solution)/shard_map/all_to_all | solution.py:17
  108.4 31.5 %all-to-all-start.1 = ((f32[32,8,14]{2,1,0:T(8,128)}), f32[32,8,14]{2,1,0:T(8,128)S(1)}, u32[]{:S(2)}, u32[]{:S(2)}) async-start(f32[32,8,14]{2,1,0:T(8,128)} %copy.22), calls=%async_computation.1 | async-start | bytes 262144 | tf_op jit(solution)/shard_map/all_to_all | solution.py:17
Sparse Core Ops, SparseCore 0:
  10.1 58.8 all-gather.1
where the time goes:
time: 148 us; the launch traced here: 147 us
  waiting for transfers between devices  70.9 us (48%)
  other arithmetic  25 us (17%)
  starting transfers between devices  20 us (14%)
  between operations  14.3 us (10%)
  local copies, waits for them, and re-layouts  11.5 us (8%)
  matrix products  5.57 us (4%)
    all_gather x1, waiting for transfers between devices, local(): segment = lax.all_gather(references, 'ref', axis=0, tiled=True)  47.2 us
    all_to_all x2, waiting for transfers between devices, sum_at_owner(): lax.all_to_all(in_blocks(shard, dim, length), axis, 0, 0, tiled=True)  23 us
    all_to_all x2, starting transfers between devices, sum_at_owner(): lax.all_to_all(in_blocks(shard, dim, length), axis, 0, 0, tiled=True)  19.9 us
    convert_element_type x1, other arithmetic, local(): wide = segment.astype(jnp.float32)  10.2 us
    reduce_sum x1, other arithmetic, local(): jnp.sum(noise_weight[None, :] * (wide[:, :coef_total] * wide[:, :coef_tot...  6.08 us
    sub x1, other arithmetic, aligned_stack(): real_part[:, None, :] * cosine_table[None]  4 us
    add x1, local copies, waits for them, and re-layouts, aligned_stack(): real_part[:, None, :] * sine_table[None]  3.22 us
  transfers between devices with their start and end apart: 3, of which 3 were waited for; matrix products, arithmetic and copies ran while one was open for 10% of the time, Pallas kernels for 0%

commit v1 on v0

--- a/solution.py
+++ b/solution.py
@@ -5,6 +5,11 @@
 from jax.sharding import PartitionSpec as P
 
 SHIFTS = 9
+
+
+def gather_over(array, name, dim):
+    outgoing = jnp.stack([array] * lax.axis_size(name))
+    return jnp.concatenate(lax.all_to_all(outgoing, name, 0, 0), axis=dim)
 
 
 def in_blocks(shard, dim, length):
@@ -101,7 +106,7 @@
     prior = jnp.dot(class_table, class_logprior, precision=lax.Precision.HIGHEST) + jnp.dot(
         orient_table, orient_logprior, precision=lax.Precision.HIGHEST
     )
-    segment = lax.all_gather(references, "ref", axis=0, tiled=True)
+    segment = gather_over(references, "ref", 0)
     cross_piece = contract(scaled_real, segment[:, :coef_total]) + contract(
         scaled_imag, segment[:, coef_total:]
     )

time: 148 us -> 204 us (1.38)
  waiting for transfers between devices: 70.9 us -> 125 us
  between operations: 14.3 us -> 0.94 us
  starting transfers between devices: 20 us -> 30.1 us
  matrix products: 5.57 us -> 9.68 us
  local copies, waits for them, and re-layouts: 11.5 us -> 13.7 us
    all_to_all x0 -> x1, waiting for transfers between devices: none -> 102 us  [gather_over(): return jnp.concatenate(lax.all_to_all(outgoing, name, 0, 0), axis=dim)]
    all_gather x1 -> x0, waiting for transfers between devices: 47.2 us -> none  [local(): segment = lax.all_gather(references, 'ref', axis=0, tiled=True)]
    all_to_all x0 -> x1, starting transfers between devices: none -> 5.59 us  [gather_over(): return jnp.concatenate(lax.all_to_all(outgoing, name, 0, 0), axis=dim)]
    another operation x0 -> x1, local copies, waits for them, and re-layouts: none -> 4.9 us  [gather_over(): outgoing = jnp.stack([array] * lax.axis_size(name))]
    all_to_all x2, starting transfers between devices: 19.9 us -> 24.5 us  [sum_at_owner(): lax.all_to_all(in_blocks(shard, dim, length), axis, 0, 0, tiled=True)]
    dot_general x2, matrix products: 2.82 us -> 6.93 us  [contract(): lax.dot_general(left, right, (((1,), (1,)), ((), ())), preferred_element_...]
  transfers between devices with their start and end apart: 3 -> 3, of which waited for: 3 -> 3; matrix products, arithmetic and copies ran while one was open for 10% -> 7% of each run, Pallas kernels for 0% -> 0%
where the time goes in v1:
time: 204 us
  waiting for transfers between devices  125 us (61%)
  starting transfers between devices  30.1 us (15%)
  other arithmetic  24.4 us (12%)
  local copies, waits for them, and re-layouts  13.7 us (7%)
  matrix products  9.68 us (5%)
    all_to_all x1, waiting for transfers between devices, gather_over(): return jnp.concatenate(lax.all_to_all(outgoing, name, 0, 0), axis=dim)  102 us
    all_to_all x2, starting transfers between devices, sum_at_owner(): lax.all_to_all(in_blocks(shard, dim, length), axis, 0, 0, tiled=True)  24.5 us
    all_to_all x2, waiting for transfers between devices, sum_at_owner(): lax.all_to_all(in_blocks(shard, dim, length), axis, 0, 0, tiled=True)  23 us
    convert_element_type x1, other arithmetic, local(): wide = segment.astype(jnp.float32)  10.2 us
    dot_general x2, matrix products, contract(): lax.dot_general(left, right, (((1,), (1,)), ((), ())), preferred_element_...  6.93 us
    reduce_sum x1, other arithmetic, local(): jnp.sum(noise_weight[None, :] * (wide[:, :coef_total] * wide[:, :coef_tot...  6.08 us
    all_to_all x1, starting transfers between devices, gather_over(): return jnp.concatenate(lax.all_to_all(outgoing, name, 0, 0), axis=dim)  5.59 us
    another operation x1, local copies, waits for them, and re-layouts, gather_over(): outgoing = jnp.stack([array] * lax.axis_size(name))  4.9 us
  transfers between devices with their start and end apart: 3, of which 3 were waited for; matrix products, arithmetic and copies ran while one was open for 7% of the time, Pallas kernels for 0%

profile of v1, /device:TPU:32, one launch (start us, length us, event | category | flops | bytes accessed | tf_op | source)
XLA Modules:
  0.0 203.9 jit_solution(12452139134189205153)
XLA Ops:
  0.6 0.0 copy-start
  0.6 4.9 %stack.2 = bf16[16,32,7168]{2,1,0:T(8,128)(2,1)} broadcast(bf16[32,7168]{1,0:T(8,128)(2,1)} %param.10), dimensions={1,2} | broadcast | bytes 7798784 | tf_op jit(solution)/shard_map/stack | solution.py:11
  5.5 5.6 %all-to-all-start = ((bf16[16,32,7168]{2,1,0:T(8,128)(2,1)}), bf16[16,32,7168]{2,1,0:T(8,128)(2,1)}, u32[]{:S(2)}, u32[]{:S(2)}) async-start(bf16[16,32,7168]{2,1,0:T(8,128)(2,1)} %stack.2), calls=%async_computation | async-start | bytes 14680064 | tf_op jit(solution)/shard_map/all_to_all | solution.py:12
  11.2 0.1 sub.250
  11.3 0.1 sub.241
  11.4 0.1 sub.251
  11.5 0.1 sub.246
  11.6 0.1 sub.236
  11.6 0.1 sub.247
  11.8 1.6 fusion.23
  13.4 4.1 %multiply_subtract_fusion = (f32[16,9,3584]{2,1,0:T(8,128)}, f32[16,9,3584]{2,1,0:T(8,128)}) fusion(f32[9,3584]{1,0:T(8,128)S(1)} %get-tuple-element.20, f32[16,3584]{1,0:T(8,128)S(1)} %get-tuple-element.17, f32[9,3584]{1,0:T(8,128)S(1)} %get-tuple-element.21, f32[16,3584]{1,0:T(8,128)S(1)} %get-tuple-element.16), kind=kLoop, calls=%fused_computation.12 | loop fusion | flops 3096576 | bytes 4845568 | tf_op jit(solution)/shard_map/sub | solution.py:55
  17.5 3.2 %add.202 = f32[144,3584]{1,0:T(8,128)} reshape(f32[16,9,3584]{2,1,0:T(8,128)} %get-tuple-element.15) | data formatting | bytes 4128768 | tf_op jit(solution)/shard_map/add | solution.py:58
  20.7 2.3 %sub.231 = f32[144,3584]{1,0:T(8,128)S(1)} reshape(f32[16,9,3584]{2,1,0:T(8,128)} %get-tuple-element.14) | data formatting | bytes 4128768 | tf_op jit(solution)/shard_map/sub | solution.py:55
  23.0 0.1 fusion.29
  23.2 0.3 fusion.13
  23.5 102.1 %all-to-all-done = bf16[16,32,7168]{2,1,0:T(8,128)(2,1)} async-done(((bf16[16,32,7168]{2,1,0:T(8,128)(2,1)}), bf16[16,32,7168]{2,1,0:T(8,128)(2,1)}, u32[]{:S(2)}, u32[]{:S(2)}) %all-to-all-start) | async-done | bytes 7340064 | tf_op jit(solution)/shard_map/all_to_all | solution.py:12
  125.6 10.2 %convert_element_type.131 = f32[512,7168]{1,0:T(8,128)} convert(bf16[512,7168]{1,0:T(8,128)(2,1)} %bitcast.8) | non-fusion elementwise | flops 3670016 | bytes 22020096 | tf_op jit(solution)/shard_map/convert_element_type | solution.py:113
  135.8 6.1 %fusion.2 = f32[512]{0:T(512)S(1)} fusion(f32[512,7168]{1,0:T(8,128)} %convert_element_type.131, f32[3584]{0:T(1024)S(1)} %copy-done.4), kind=kLoop, calls=%fused_computation.3 | loop fusion | flops 9174528 | bytes 14696448 | tf_op jit(solution)/shard_map/reduce_sum | solution.py:114
  141.9 3.4 %fusion.3 = f32[144,512]{1,0:T(8,128)S(1)} fusion(bf16[512,7168]{1,0:T(8,128)(2,1)} %bitcast.8, f32[144,3584]{1,0:T(8,128)S(1)} %copy-done.2, f32[3584]{0:T(1024)S(1)} %broadcast_multiply_fusion), kind=kOutput, calls=%fused_computation.7 | convolution fusion | flops 529514496 | bytes 6043648 | tf_op jit(solution)/shard_map/dot_general | solution.py:75
  145.3 3.5 %fusion.16 = (f32[144]{0:T(256)S(1)}, f32[144,512]{1,0:T(8,128)S(1)}) fusion(f32[144]{0:T(256)S(1)} %add_multiply_fusion.2, f32[512]{0:T(512)S(1)} %add.205, f32[512]{0:T(512)S(1)} %fusion.2, f32[144,512]{1,0:T(8,128)S(1)} %fusion.3, bf16[512,7168]{1,0:T(8,128)(2,1)} %bitcast.8, f32[144,3584]{1,0:T(8,128)S(1)} %sub.231, f32[3584]{0:T(1024)S(1)} %broadcast_multiply_fusion), kind=kOutput, calls=%fused_computation.34 | convolution fusion | flops 529883008 | bytes 6343808 | tf_op jit(solution)/shard_map/dot_general | solution.py:75
  148.9 0.0 copy-start.3
  148.9 0.1 reduce_max.14
  149.0 0.1 reduce_max.18
  149.1 0.1 sub.253
  149.1 0.1 sub.254
  149.2 0.2 exponential_reduce_fusion
  149.5 0.1 reduce_sum.45
  149.6 0.1 reduce_sum.46
  149.7 0.1 sub.259
  149.8 0.1 sub.260
  149.9 0.1 subtract_exponential_fusion
  150.1 1.0 fusion.34
  151.1 0.1 copy.19
  151.2 0.5 convolution_bitcast_fusion
  151.8 0.7 multiply_reduce_fusion.3
  152.6 0.1 concatenate.9
  152.7 0.1 concatenate.8
  152.8 0.9 fusion.12
  153.7 6.8 %all-to-all-start.1 = ((f32[16,8,448]{2,1,0:T(8,128)}), f32[16,8,448]{2,1,0:T(8,128)S(1)}, u32[]{:S(2)}, u32[]{:S(2)}) async-start(f32[16,8,448]{2,1,0:T(8,128)} %fusion.12), calls=%async_computation.1 | async-start | bytes 524288 | tf_op jit(solution)/shard_map/all_to_all | solution.py:22
  160.5 0.1 add_multiply_fusion.1
  160.6 7.5 %all-to-all-done.1 = f32[16,8,448]{2,1,0:T(8,128)S(1)} async-done(((f32[16,8,448]{2,1,0:T(8,128)}), f32[16,8,448]{2,1,0:T(8,128)S(1)}, u32[]{:S(2)}, u32[]{:S(2)}) %all-to-all-start.1) | async-done | bytes 229408 | tf_op jit(solution)/shard_map/all_to_all | solution.py:22
  168.2 0.1 reshape.313
  168.3 0.7 copy.22
  169.1 17.7 %all-to-all-start.2 = ((f32[32,8,14]{2,1,0:T(8,128)}), f32[32,8,14]{2,1,0:T(8,128)S(1)}, u32[]{:S(2)}, u32[]{:S(2)}) async-start(f32[32,8,14]{2,1,0:T(8,128)} %copy.22), calls=%async_computation.2 | async-start | bytes 262144 | tf_op jit(solution)/shard_map/all_to_all | solution.py:22
  186.8 0.1 add_subtract_fusion
  186.9 0.9 copy.23
  187.8 15.4 %all-to-all-done.2 = f32[32,8,14]{2,1,0:T(8,128)S(1)} async-done(((f32[32,8,14]{2,1,0:T(8,128)}), f32[32,8,14]{2,1,0:T(8,128)S(1)}, u32[]{:S(2)}, u32[]{:S(2)}) %all-to-all-start.2) | async-done | bytes 14368 | tf_op jit(solution)/shard_map/all_to_all | solution.py:22
  203.2 0.6 reduce_sum.48
  (32 shorter events, 0.3 us)
Async XLA Ops:
  0.6 22.4 %copy-start = (f32[8]{0:T(128)S(1)}, f32[8]{0:T(128)}, u32[]{:S(2)}) copy-start(f32[8]{0:T(128)} %param.14) | copy-start | bytes 100
  5.5 5.7 %copy-start.7 = (s32[16]{0:T(128)S(1)}, s32[16]{0:T(128)}, u32[]{:S(2)}) copy-start(s32[16]{0:T(128)} %param.9) | copy-start | bytes 196
  5.5 6.2 %copy-start.1 = (bf16[16,7168]{1,0:T(8,128)(2,1)S(1)}, bf16[16,7168]{1,0:T(8,128)(2,1)}, u32[]{:S(2)}) copy-start(bf16[16,7168]{1,0:T(8,128)(2,1)} %param.8) | copy-start | bytes 688132
  5.5 120.1 %all-to-all-start = ((bf16[16,32,7168]{2,1,0:T(8,128)(2,1)}), bf16[16,32,7168]{2,1,0:T(8,128)(2,1)}, u32[]{:S(2)}, u32[]{:S(2)}) async-start(bf16[16,32,7168]{2,1,0:T(8,128)(2,1)} %stack.2), calls=%async_computation | async-start | bytes 14680064 | tf_op jit(solution)/shard_map/all_to_all | solution.py:12
  20.7 2.3 %copy-start.5 = (s32[512]{0:T(512)S(1)}, s32[512]{0:T(512)}, u32[]{:S(2)}) copy-start(s32[512]{0:T(512)} %param.12) | copy-start | bytes 6148
  20.7 2.5 %copy-start.6 = (s32[512]{0:T(512)S(1)}, s32[512]{0:T(512)}, u32[]{:S(2)}) copy-start(s32[512]{0:T(512)} %param.13) | copy-start | bytes 6148
  20.7 2.5 %copy-start.8 = (f32[64]{0:T(128)S(1)}, f32[64]{0:T(128)}, u32[]{:S(2)}) copy-start(f32[64]{0:T(128)} %param.15) | copy-start | bytes 772
  20.7 2.8 %copy-start.4 = (f32[3584]{0:T(1024)S(1)}, f32[3584]{0:T(1024)}, u32[]{:S(2)}) copy-start(f32[3584]{0:T(1024)} %param.11) | copy-start | bytes 43012
  135.8 6.1 %copy-start.2 = (f32[144,3584]{1,0:T(8,128)S(1)}, f32[144,3584]{1,0:T(8,128)}, u32[]{:S(2)}) copy-start(f32[144,3584]{1,0:T(8,128)} %add.202) | copy-start | bytes 6193156
  148.9 2.9 %copy-start.3 = (f32[3584,9]{0,1:T(8,128)S(1)}, f32[3584,9]{0,1:T(8,128)}, u32[]{:S(2)}) copy-start(f32[3584,9]{0,1:T(8,128)} %get-tuple-element.19) | copy-start | bytes 387076
  153.7 14.5 %all-to-all-start.1 = ((f32[16,8,448]{2,1,0:T(8,128)}), f32[16,8,448]{2,1,0:T(8,128)S(1)}, u32[]{:S(2)}, u32[]{:S(2)}) async-start(f32[16,8,448]{2,1,0:T(8,128)} %fusion.12), calls=%async_computation.1 | async-start | bytes 524288 | tf_op jit(solution)/shard_map/all_to_all | solution.py:22
  169.1 34.2 %all-to-all-start.2 = ((f32[32,8,14]{2,1,0:T(8,128)}), f32[32,8,14]{2,1,0:T(8,128)S(1)}, u32[]{:S(2)}, u32[]{:S(2)}) async-start(f32[32,8,14]{2,1,0:T(8,128)} %copy.22), calls=%async_computation.2 | async-start | bytes 262144 | tf_op jit(solution)/shard_map/all_to_all | solution.py:22
